TPU v7x, 32 devices: a whole 2x2x4 slice. The times are simulated.
32 devices in a mesh: rows: 8 (over z, x), rep: 4 (over y, core).
Axes of the slice: x: 2, y: 2, z: 4, core: 2. Of those that a mesh axis runs over, the one named last changes fastest.
Arguments:
- requests: int32 [32, 8, 128], P(('rows', 'rep')), may hold values from 0 to 1023
- request_counts: int32 [32, 8], P(('rows', 'rep')), may hold values from 0 to 128, as said below
- table: bfloat16 [8192, 512], P('rows')
- gain: float32 [512], replicated, may hold values from 0.5 to 1.5
Outputs:
- normalized: bfloat16 [32, 8, 128, 512], P(('rows', 'rep'))
- row_counts: int32 [8192], P('rows')
- moments: float32 [2, 2], replicated
Inputs may be any that keep to these rules, and one draw needn't show every extreme that they name: Each device uses request_counts[d, o] of its 128 slots toward owner o; in every draw one owner's slots are full from every device.
All inputs are finite; a program needn't handle non-finite values.
Results may differ from a plain program's by a relative error of at most 0.0004.
Values may be sent and summed in bfloat16 or wider, within the bound.
No kernel may reach another device: no remote copies, remote signals or barrier semaphores. Data moves between devices by JAX's collectives and lax.ppermute only.
A program may use at most 64 MiB of HBM per device.

v0:
```python
import jax
import jax.numpy as jnp
from jax import lax
from jax.sharding import PartitionSpec as P

WIDTH = 256
LAYERS = 2


epsilon = 1e-06


def joined(part, axis, combine):
    gathered = jax.tree.map(lambda a: lax.all_gather(a, axis), part)

    def take(source):
        return jax.tree.map(lambda a: lax.dynamic_index_in_dim(a, source, 0, False), gathered)

    return lax.fori_loop(
        1, lax.axis_size(axis), lambda source, state: combine(state, take(source)), take(0)
    )


def merge_moments(former, latter):
    count_former, mean_former, square_former = former
    count_latter, mean_latter, square_latter = latter
    merged_count = count_former + count_latter
    safe_count = jnp.maximum(merged_count, 1.0)
    delta_mean = mean_latter - mean_former
    merged_mean = mean_former + delta_mean * count_latter / safe_count
    merged_square = (
        square_former
        + square_latter
        + delta_mean * delta_mean * count_former * count_latter / safe_count
    )
    return (merged_count, merged_mean, merged_square)


def per_device(requests, request_counts, table, gain):
    wanted, wanted_counts = (
        lax.all_to_all(requests, "rows", split_axis=1, concat_axis=0, tiled=True),
        lax.all_to_all(request_counts, "rows", split_axis=1, concat_axis=0, tiled=True),
    )
    owners = wanted.shape[0]
    slot_count = wanted.shape[2]
    held_rows = table.shape[0]
    row_index = wanted.reshape(-1)
    live_slot = lax.broadcasted_iota(jnp.int32, (owners, slot_count), 1) < wanted_counts
    live_flat = live_slot.reshape(-1)
    matches = (row_index[:, None] == jnp.arange(held_rows, dtype=jnp.int32)[None, :]) & live_flat[
        :, None
    ]
    local_counts = jnp.sum(matches.astype(jnp.int32), axis=0)
    row_counts = lax.psum(local_counts, "rep")
    shaped = table.reshape(held_rows, LAYERS, WIDTH)
    weights = row_counts.astype(jnp.float32)
    partial_value = jnp.dot(
        weights, jnp.sum(shaped, axis=2, dtype=jnp.float32), precision=lax.Precision.HIGHEST
    )
    count_layers = jnp.full((LAYERS,), jnp.sum(weights) * WIDTH, jnp.float32)
    mean_here = partial_value / jnp.maximum(count_layers, 1.0)
    centered = jnp.sum(jnp.square(shaped.astype(jnp.float32) - mean_here[None, :, None]), axis=2)
    square_here = jnp.dot(weights, centered, precision=lax.Precision.HIGHEST)
    entries, layer_mean, merged_square = joined(
        (count_layers, mean_here, square_here), "rows", merge_moments
    )
    layer_var = merged_square / entries
    inverse = jnp.repeat(lax.rsqrt(layer_var + epsilon), WIDTH) * gain
    mean_full = jnp.repeat(layer_mean, WIDTH)
    looked = jnp.take(table, row_index, axis=0).reshape(owners, 1, slot_count, LAYERS * WIDTH)
    scaled = (looked.astype(jnp.float32) - mean_full) * inverse
    scaled = jnp.where(live_slot.reshape(owners, 1, slot_count, 1), scaled, 0.0).astype(
        jnp.bfloat16
    )
    normalized = lax.all_to_all(scaled, "rows", split_axis=0, concat_axis=1, tiled=True)
    return (normalized, row_counts, jnp.stack([layer_mean, layer_var]))


def solution(mesh):
    return jax.shard_map(
        per_device,
        mesh=mesh,
        in_specs=(P(("rows", "rep"), None, None), P(("rows", "rep"), None), P("rows", None), P()),
        out_specs=(P(("rows", "rep"), None, None, None), P("rows"), P()),
        check_vma=False,
    )
```

profile of v0, /device:TPU:0, one launch (start us, length us, event | category | flops | bytes accessed | tf_op | source)
XLA Modules:
  0.0 89.4 jit_solution(5345991908360352691)
XLA Ops:
  0.6 1.3 %copy.13 = s32[1,8,1]{2,0,1:T(1,128)} copy(s32[1,8,1]{1,2,0:T(1,128)} %bitcast.86) | data formatting | bytes 64 | tf_op jit(solution)/shard_map/all_to_all | solution.py:42
  2.0 7.3 %all-to-all-start = ((s32[1,8,1]{2,0,1:T(1,128)}), s32[1,8,1]{2,0,1:T(1,128)S(1)}, u32[]{:S(2)}, u32[]{:S(2)}) async-start(s32[1,8,1]{2,0,1:T(1,128)} %copy.13), calls=%async_computation | async-start | bytes 8192 | tf_op jit(solution)/shard_map/all_to_all | solution.py:42
  9.2 2.4 %reshape.157 = f32[1024,2,256]{2,1,0:T(2,128)S(1)} reshape(bf16[1024,512]{1,0:T(8,128)(2,1)} %param.8) | data formatting | bytes 3145728 | tf_op jit(solution)/shard_map/convert_element_type | solution.py:58
  11.6 0.0 copy-start.3
  11.6 1.9 %reduce_sum.38 = f32[1024,2]{1,0:T(8,128)} reduce(f32[1024,2,256]{2,1,0:T(2,128)S(1)} %reshape.157, f32[]{:T(128)} %constant.79.clone.1), dimensions={2}, to_apply=%region_3.0 | reduce | flops 522240 | bytes 2105348 | tf_op jit(solution)/shard_map/reduce_sum | solution.py:58
  13.6 0.0 copy-start
  13.6 0.0 copy-done.3
  13.6 0.7 dynamic-slice
  14.9 0.7 all-to-all-done
  15.7 5.3 %all-to-all-start.1 = ((s32[1,8,128]{2,0,1:T(1,128)}), s32[1,8,128]{2,0,1:T(1,128)S(1)}, u32[]{:S(2)}, u32[]{:S(2)}) async-start(s32[1,8,128]{2,0,1:T(1,128)} %bitcast.4), calls=%async_computation.1 | async-start | bytes 8192 | tf_op jit(solution)/shard_map/all_to_all | solution.py:41
  20.9 0.2 reduce
  21.2 0.1 iota_compare_fusion.1
  21.3 6.1 %all-to-all-done.1 = s32[1,8,128]{2,0,1:T(1,128)S(1)} async-done(((s32[1,8,128]{2,0,1:T(1,128)}), s32[1,8,128]{2,0,1:T(1,128)S(1)}, u32[]{:S(2)}, u32[]{:S(2)}) %all-to-all-start.1) | async-done | bytes 4128 | tf_op jit(solution)/shard_map/all_to_all | solution.py:41
  27.4 0.8 convert_reduce_fusion
  28.1 5.0 %psum.7 = s32[1024]{0:T(1024)S(1)} all-reduce(s32[1024]{0:T(1024)S(1)} %convert_reduce_fusion), channel_id=1, replica_groups=mesh['rows'=8,'rep'=4] {'rep'}, use_global_device_ids=true, to_apply=%region_1.0 | all-reduce | flops 1024 | bytes 8192 | tf_op jit(solution)/shard_map/psum | solution.py:54
  33.1 0.0 copy-start.1
  33.1 0.6 convert_reduce_fusion.1
  34.4 1.4 %fusion.8 = f32[2]{0:T(128)S(1)} fusion(f32[1024,1]{0,1:T(1,128)S(1)} %bitcast.77, f32[1024,2]{1,0:T(8,128)} %reduce_sum.38, f32[]{:T(128)S(6)} %max.14), kind=kOutput, calls=%fused_computation.19 | convolution fusion | flops 24578 | bytes 12300 | tf_op jit(solution)/shard_map/dot_general | solution.py:57
  35.8 1.3 %multiply_reduce_fusion = f32[1024,2]{1,0:T(8,128)S(1)} fusion(f32[1024,2,256]{2,1,0:T(2,128)S(1)} %reshape.157, f32[2]{0:T(128)S(1)} %fusion.8), kind=kLoop, calls=%fused_computation.16 | loop fusion | flops 1570816 | bytes 2105352 | tf_op jit(solution)/shard_map/reduce_sum | solution.py:62
  37.0 0.4 convolution_bitcast_fusion
  37.4 0.2 dynamic-update-slice.1
  37.6 0.2 dynamic-update-slice.2
  37.8 0.8 dynamic-update-slice
  38.6 17.7 %all-reduce.3 = (f32[8]{0:T(128)S(1)}, f32[16]{0:T(128)S(1)}, f32[16]{0:T(128)S(1)}) all-reduce(f32[8]{0:T(128)S(1)} %dynamic-update-slice, f32[16]{0:T(128)S(1)} %dynamic-update-slice.1, f32[16]{0:T(128)S(1)} %dynamic-update-slice.2), channel_id=2, replica_groups=mesh['rows'=8,'rep'=4] {'rows'}, use_global_device_ids=true, to_apply=%add | all-reduce | flops 40 | bytes 320
  56.3 0.1 reshape.168
  56.4 0.1 reshape.169
  56.5 0.1 broadcast.115
  56.6 0.5 while.19
  57.1 0.1 broadcast_bitcast_fusion
  57.2 0.1 broadcast_bitcast_fusion.1
  57.3 0.0 copy-done
  57.3 0.0 copy-start.2
  57.3 4.0 %gather_fusion = bf16[1024,512]{1,0:T(8,128)(2,1)S(1)} fusion(bf16[1024,512]{1,0:T(8,128)(2,1)S(1)} %copy-done, s32[1024]{0:T(1024)S(1)} %broadcast_clamp_fusion), kind=kCustom, calls=%fused_computation | custom fusion | bytes 2101248 | tf_op jit(solution)/shard_map/jit(_take)/gather | solution.py:70
  61.3 0.0 copy-done.1
  61.3 0.0 copy-done.2
  61.3 1.8 %select_convert_fusion = bf16[8,1,128,512]{3,2,1,0:T(8,128)(2,1)} fusion(f32[512]{0:T(512)S(1)} %mul.63, f32[512]{0:T(512)S(1)} %bitcast.83, bf16[8,1,128,512]{3,2,1,0:T(8,128)(2,1)S(1)} %bitcast.73, pred[8,128]{1,0:T(8,128)(4,1)S(1)} %compare_and_fusion, pred[8,128]{1,0:T(8,128)(4,1)S(1)} %get-tuple-element.205), kind=kLoop, calls=%fused_computation.15 | loop fusion | flops 3145728 | bytes 2103296 | tf_op jit(solution)/shard_map/convert_element_type | solution.py:72
  63.1 3.6 %all-to-all-start.2 = ((bf16[8,1,128,512]{3,2,1,0:T(8,128)(2,1)}), bf16[8,1,128,512]{3,2,1,0:T(8,128)(2,1)S(1)}, u32[]{:S(2)}, u32[]{:S(2)}) async-start(bf16[8,1,128,512]{3,2,1,0:T(8,128)(2,1)} %select_convert_fusion), calls=%async_computation.2 | async-start | bytes 2097152 | tf_op jit(solution)/shard_map/all_to_all | solution.py:75
  66.6 0.6 pad_maximum_fusion
  67.2 21.2 %all-to-all-done.2 = bf16[8,1,128,512]{3,2,1,0:T(8,128)(2,1)S(1)} async-done(((bf16[8,1,128,512]{3,2,1,0:T(8,128)(2,1)}), bf16[8,1,128,512]{3,2,1,0:T(8,128)(2,1)S(1)}, u32[]{:S(2)}, u32[]{:S(2)}) %all-to-all-start.2) | async-done | bytes 1048608 | tf_op jit(solution)/shard_map/all_to_all | solution.py:75
  88.4 1.0 %copy.35 = bf16[1,8,128,512]{3,2,1,0:T(8,128)(2,1)} copy(bf16[1,8,128,512]{3,2,1,0:T(8,128)(2,1)S(1)} %bitcast.74) | data formatting | bytes 2097152
  (26 shorter events, 0.4 us)
Async XLA Ops:
  2.0 13.7 %all-to-all-start = ((s32[1,8,1]{2,0,1:T(1,128)}), s32[1,8,1]{2,0,1:T(1,128)S(1)}, u32[]{:S(2)}, u32[]{:S(2)}) async-start(s32[1,8,1]{2,0,1:T(1,128)} %copy.13), calls=%async_computation | async-start | bytes 8192 | tf_op jit(solution)/shard_map/all_to_all | solution.py:42
  11.6 2.0 %copy-start.3 = (u32[32]{0:T(128)S(1)}, u32[32]{0:T(128)}, u32[]{:S(2)}) copy-start(u32[32]{0:T(128)} %constant.87) | copy-start | bytes 388
  13.6 43.7 %copy-start = (bf16[1024,512]{1,0:T(8,128)(2,1)S(1)}, bf16[1024,512]{1,0:T(8,128)(2,1)}, u32[]{:S(2)}) copy-start(bf16[1024,512]{1,0:T(8,128)(2,1)} %param.8) | copy-start | bytes 3145732
  15.7 11.7 %all-to-all-start.1 = ((s32[1,8,128]{2,0,1:T(1,128)}), s32[1,8,128]{2,0,1:T(1,128)S(1)}, u32[]{:S(2)}, u32[]{:S(2)}) async-start(s32[1,8,128]{2,0,1:T(1,128)} %bitcast.4), calls=%async_computation.1 | async-start | bytes 8192 | tf_op jit(solution)/shard_map/all_to_all | solution.py:41
  33.1 28.2 %copy-start.1 = (s32[1024]{0:T(1024)}, s32[1024]{0:T(1024)S(1)}, u32[]{:S(2)}) copy-start(s32[1024]{0:T(1024)S(1)} %psum.7) | copy-start | bytes 12292
  57.3 4.0 %copy-start.2 = (f32[512]{0:T(512)S(1)}, f32[512]{0:T(512)}, u32[]{:S(2)}) copy-start(f32[512]{0:T(512)} %param.9) | copy-start | bytes 6148
  63.1 25.4 %all-to-all-start.2 = ((bf16[8,1,128,512]{3,2,1,0:T(8,128)(2,1)}), bf16[8,1,128,512]{3,2,1,0:T(8,128)(2,1)S(1)}, u32[]{:S(2)}, u32[]{:S(2)}) async-start(bf16[8,1,128,512]{3,2,1,0:T(8,128)(2,1)} %select_convert_fusion), calls=%async_computation.2 | async-start | bytes 2097152 | tf_op jit(solution)/shard_map/all_to_all | solution.py:75
where the time goes:
time: 89.8 us; the launch traced here: 89.4 us
  waiting for transfers between devices  28.1 us (31%)
  blocking collectives  22.6 us (25%)
  starting transfers between devices  16.1 us (18%)
  local copies, waits for them, and re-layouts  11 us (12%)
  other arithmetic  7.57 us (8%)
  between operations  2.13 us (2%)
  matrix products  1.75 us (2%)
    all_to_all x1, waiting for transfers between devices, per_device(): lax.all_to_all(scaled, 'rows', split_axis=0, concat_axis=1, tiled=True)  21.2 us
    unnamed x1, blocking collectives  17.7 us
    all_to_all x1, starting transfers between devices, per_device(): lax.all_to_all(request_counts, 'rows', split_axis=1, concat_axis=0, tiled...  7.28 us
    all_to_all x1, waiting for transfers between devices, per_device(): lax.all_to_all(requests, 'rows', split_axis=1, concat_axis=0, tiled=True)  6.11 us
    all_to_all x1, starting transfers between devices, per_device(): lax.all_to_all(requests, 'rows', split_axis=1, concat_axis=0, tiled=True)  5.29 us
    psum x1, blocking collectives, per_device(): row_counts = lax.psum(local_counts, 'rep')  4.97 us
    gather x1, local copies, waits for them, and re-layouts, per_device(): jnp.take(table, row_index, axis=0)  3.97 us
    all_to_all x1, starting transfers between devices, per_device(): lax.all_to_all(scaled, 'rows', split_axis=0, concat_axis=1, tiled=True)  3.56 us
  transfers between devices with their start and end apart: 3, of which 3 were waited for; matrix products, arithmetic and copies ran while one was open for 7% of the time, Pallas kernels for 0%

commit v1 on v0

v1 whole, which is shorter than its diff:
```python
import functools

import jax
import jax.numpy as jnp
from jax import lax
from jax.experimental import pallas as pl
from jax.experimental.pallas import tpu as pltpu
from jax.sharding import PartitionSpec as P

WIDTH = 256
LAYERS = 2
LANES = 128
SUBLANES = 8

epsilon = 1e-06


def row_moments_kernel(table_ref, moments_ref):
    blocks = table_ref.shape[0] // LANES
    lane = lax.broadcasted_iota(jnp.int32, (LANES, LANES), 1)
    columns = jnp.zeros((LANES, LANES), jnp.float32)
    for block in range(blocks):
        for layer in range(LAYERS):
            x = table_ref[
                block * LANES : (block + 1) * LANES, layer * WIDTH : (layer + 1) * WIDTH
            ].astype(jnp.float32)
            mean = jnp.sum(x, axis=1, keepdims=True) * (1.0 / WIDTH)
            square = jnp.sum(jnp.square(x - mean), axis=1, keepdims=True)
            columns = jnp.where(lane == layer * blocks + block, mean, columns)
            columns = jnp.where(lane == (LAYERS + layer) * blocks + block, square, columns)
    moments_ref[...] = jnp.transpose(columns)[: 2 * LAYERS * blocks]


def serve_kernel(slot_count, mine_ref, wanted_ref, moments_ref, table_ref, payload_ref, counts_ref, high_ref, low_ref):
    held_rows, columns = table_ref.shape
    blocks = held_rows // LANES
    requests = wanted_ref.shape[0]
    lane = lax.broadcasted_iota(jnp.int32, (LANES, LANES), 1)
    block_row = lax.broadcasted_iota(jnp.int32, (blocks, LANES), 0)
    one, nought = jnp.bfloat16(1), jnp.bfloat16(0)

    wanted = wanted_ref[...]
    upright = jnp.transpose(wanted)
    for row in range(requests):
        span = slice(row * LANES, (row + 1) * LANES)
        high = wanted[row : row + 1] // LANES
        low = upright[:, row : row + 1] % LANES
        high_ref[:, span] = jnp.where(block_row == high, 1.0, 0.0).astype(jnp.bfloat16)
        low_ref[span, :] = jnp.where(lane == low, 1.0, 0.0).astype(jnp.bfloat16)
    weights = jnp.dot(high_ref[...], low_ref[...], preferred_element_type=jnp.float32)
    counts_ref[...] = weights.astype(jnp.int32)

    tile_row = lax.broadcasted_iota(jnp.int32, (SUBLANES, LANES), 0)
    tile_lane = lax.broadcasted_iota(jnp.int32, (SUBLANES, LANES), 1)

    def total(a):
        return jnp.sum(jnp.sum(a, axis=1, keepdims=True), axis=0, keepdims=True)

    count = total(weights)
    figures = jnp.where(tile_lane == 0, count, 0.0)
    for layer in range(LAYERS):
        row_mean = moments_ref[layer * blocks : (layer + 1) * blocks]
        row_square = moments_ref[(LAYERS + layer) * blocks : (LAYERS + layer + 1) * blocks]
        mean = total(weights * row_mean) / jnp.maximum(count, 1.0)
        square = total(weights * (row_square + WIDTH * jnp.square(row_mean - mean)))
        figures = jnp.where(tile_lane == 1 + layer, mean, figures)
        figures = jnp.where(tile_lane == 1 + LAYERS + layer, square, figures)
    first = figures.astype(jnp.bfloat16).astype(jnp.float32)
    second = (figures - first).astype(jnp.bfloat16).astype(jnp.float32)
    third = figures - first - second
    terms = jnp.where(tile_row == 0, first, jnp.where(tile_row == 1, second, third)).astype(jnp.bfloat16)

    pieces = columns // LANES
    owned = mine_ref.shape[0]
    peers = payload_ref.shape[0]
    mine = jnp.transpose(mine_ref[...])
    row_lane = lax.broadcasted_iota(jnp.int32, (LANES, held_rows), 1)
    for row in range(owned):
        chosen = jnp.where(row_lane == mine[:, row : row + 1], 1.0, 0.0).astype(jnp.bfloat16)
        rows = jnp.dot(chosen, table_ref[...], preferred_element_type=jnp.float32)
        for start in range(0, LANES, slot_count):
            peer = (row * LANES + start) // slot_count
            for piece in range(pieces):
                payload_ref[peer, piece * slot_count : (piece + 1) * slot_count, :] = rows[
                    start : start + slot_count, piece * LANES : (piece + 1) * LANES
                ].astype(jnp.bfloat16)
    for peer in range(peers):
        payload_ref[peer, pieces * slot_count :, :] = terms


def normalize_kernel(used_ref, received_ref, gain_ref, out_ref, moments_ref, ready_ref, sems):
    owners, slot_count, columns = out_ref.shape
    pieces = columns // LANES
    count = jnp.zeros((1, LANES), jnp.float32)
    tail = [
        received_ref[owner, pieces * slot_count :, :].astype(jnp.float32) for owner in range(owners)
    ]
    figures = [t[0:1] + t[1:2] + t[2:3] for t in tail]
    counts = [f[:, 0:1] for f in figures]
    entries = functools.reduce(jnp.add, counts)
    out_row = lax.broadcasted_iota(jnp.int32, moments_ref.shape, 0)
    out_lane = lax.broadcasted_iota(jnp.int32, moments_ref.shape, 1)
    summary = jnp.zeros(moments_ref.shape, jnp.float32)
    means, scales = [], []
    for layer in range(LAYERS):
        held = [f[:, 1 + layer : 2 + layer] for f in figures]
        squares = [f[:, 1 + LAYERS + layer : 2 + LAYERS + layer] for f in figures]
        mean = functools.reduce(jnp.add, [c * m for c, m in zip(counts, held)]) / entries
        square = functools.reduce(
            jnp.add, [s + WIDTH * c * jnp.square(m - mean) for c, m, s in zip(counts, held, squares)]
        )
        variance = square / (entries * WIDTH)
        means.append(mean)
        scales.append(lax.rsqrt(variance + epsilon))
        summary = jnp.where(out_lane == layer, jnp.where(out_row == 0, mean, variance), summary)
    moments_ref[...] = summary

    slot = lax.broadcasted_iota(jnp.int32, (slot_count, LANES), 0)
    copies = []
    for owner in range(owners):
        live = slot < used_ref[0, owner]
        for piece in range(pieces):
            span = slice(piece * LANES, (piece + 1) * LANES)
            layer = piece * LANES // WIDTH
            x = received_ref[owner, piece * slot_count : (piece + 1) * slot_count, :].astype(jnp.float32)
            scaled = (x - means[layer]) * (scales[layer] * gain_ref[:, span])
            ready_ref[owner, :, span] = jnp.where(live, scaled, 0.0).astype(jnp.bfloat16)
        copy = pltpu.make_async_copy(ready_ref.at[owner], out_ref.at[owner], sems.at[owner])
        copy.start()
        copies.append(copy)
    for copy in copies:
        copy.wait()


def per_device(groups, requests, request_counts, table, gain):
    _, owners, slot_count = requests.shape
    held_rows, columns = table.shape
    pieces = columns // LANES
    vmem = pl.BlockSpec(memory_space=pltpu.VMEM)
    slot = lax.broadcasted_iota(jnp.int32, (owners, slot_count), 1)
    asked = jnp.where(slot < request_counts[0][:, None], requests[0], held_rows)
    asked = jnp.broadcast_to(asked[None], (groups, owners, slot_count)).reshape(groups * owners, slot_count)
    wanted = lax.all_to_all(asked, ("rep", "rows"), split_axis=0, concat_axis=0, tiled=True)
    wanted = wanted.reshape(groups, owners * slot_count // LANES, LANES)
    mine = lax.dynamic_index_in_dim(wanted, lax.axis_index("rep"), 0, False)
    wanted = wanted.reshape(-1, LANES)
    blocks = held_rows // LANES
    moments = pl.pallas_call(
        row_moments_kernel,
        out_shape=jax.ShapeDtypeStruct((2 * LAYERS * blocks, LANES), jnp.float32),
        in_specs=[vmem],
        out_specs=vmem,
        name="row_moments",
    )(table)
    payload, row_counts = pl.pallas_call(
        functools.partial(serve_kernel, slot_count),
        out_shape=(
            jax.ShapeDtypeStruct((owners, pieces * slot_count + SUBLANES, LANES), jnp.bfloat16),
            jax.ShapeDtypeStruct((blocks, LANES), jnp.int32),
        ),
        in_specs=[vmem] * 4,
        out_specs=(vmem, vmem),
        scratch_shapes=[
            pltpu.VMEM((blocks, wanted.size), jnp.bfloat16),
            pltpu.VMEM((wanted.size, LANES), jnp.bfloat16),
        ],
        name="serve",
    )(mine, wanted, moments, table)
    received = lax.all_to_all(payload, "rows", split_axis=0, concat_axis=0, tiled=True)
    normalized, summary = pl.pallas_call(
        normalize_kernel,
        out_shape=(
            jax.ShapeDtypeStruct((owners, slot_count, columns), jnp.bfloat16),
            jax.ShapeDtypeStruct((2, LAYERS), jnp.float32),
        ),
        in_specs=[pl.BlockSpec(memory_space=pltpu.SMEM), vmem, vmem],
        out_specs=(pl.BlockSpec(memory_space=pl.ANY), vmem),
        scratch_shapes=[
            pltpu.VMEM((owners, slot_count, columns), jnp.bfloat16),
            pltpu.SemaphoreType.DMA((owners,)),
        ],
        name="normalize",
    )(request_counts, received, gain[None])
    return (normalized[None], row_counts.reshape(-1), summary)


def solution(mesh):
    return jax.shard_map(
        functools.partial(per_device, mesh.shape["rep"]),
        mesh=mesh,
        in_specs=(P(("rows", "rep"), None, None), P(("rows", "rep"), None), P("rows", None), P()),
        out_specs=(P(("rows", "rep"), None, None, None), P("rows"), P()),
        check_vma=False,
    )
```

time: 89.8 us -> 57.3 us (0.64)
  waiting for transfers between devices: 28.1 us -> 3.86 us
  Pallas kernels: 0 us -> 11.7 us
  local copies, waits for them, and re-layouts: 11 us -> 1.21 us
  blocking collectives: 22.6 us -> 31.4 us
  starting transfers between devices: 16.1 us -> 7.33 us
  other arithmetic: 7.57 us -> 0.76 us
  matrix products: 1.75 us -> 0 us
  between operations: 2.13 us -> 0.65 us
    all_to_all x0 -> x1, blocking collectives: none -> 31.4 us  [per_device(): lax.all_to_all(payload, 'rows', split_axis=0, concat_axis=0, tiled=True)]
    all_to_all x3 -> x1, waiting for transfers between devices: 28.1 us -> 3.86 us  [per_device(): lax.all_to_all(asked, ('rep', 'rows'), split_axis=0, concat_axis=0, tiled...]
    unnamed x1 -> x0, blocking collectives: 17.7 us -> none
    pallas_call x0 -> x3, Pallas kernels: none -> 11.7 us  [the longest x1 4.89 us: per_device(): pl.pallas_call(functools.partial(serve_kernel, slot_count), out_shape=(ja...]
    all_to_all x3 -> x1, starting transfers between devices: 16.1 us -> 7.33 us  [per_device(): lax.all_to_all(asked, ('rep', 'rows'), split_axis=0, concat_axis=0, tiled...]
    psum x1 -> x0, blocking collectives: 4.97 us -> none  [per_device(): row_counts = lax.psum(local_counts, 'rep')]
    reduce_sum x4 -> x0, other arithmetic: 4.58 us -> none  [the longest x1 1.95 us: per_device(): jnp.sum(shaped, axis=2, dtype=jnp.float32)]
    gather x1 -> x0, local copies, waits for them, and re-layouts: 3.97 us -> none  [per_device(): jnp.take(table, row_index, axis=0)]
  transfers between devices with their start and end apart: 3 -> 1, of which waited for: 3 -> 1; matrix products, arithmetic and copies ran while one was open for 7% -> 0% of each run, Pallas kernels for 0% -> 6%
where the time goes in v1:
time: 57.3 us; the launch traced here: 57 us
  blocking collectives  31.4 us (55%)
  Pallas kernels  11.7 us (20%)
  starting transfers between devices  7.33 us (13%)
  waiting for transfers between devices  3.86 us (7%)
  local copies, waits for them, and re-layouts  1.21 us (2%)
  other arithmetic  0.76 us (1%)
  between operations  0.65 us (1%)
    all_to_all x1, blocking collectives, per_device(): lax.all_to_all(payload, 'rows', split_axis=0, concat_axis=0, tiled=True)  31.4 us
    all_to_all x1, starting transfers between devices, per_device(): lax.all_to_all(asked, ('rep', 'rows'), split_axis=0, concat_axis=0, tiled...  7.33 us
    pallas_call x1, Pallas kernels, per_device(): pl.pallas_call(functools.partial(serve_kernel, slot_count), out_shape=(ja...  4.89 us
    all_to_all x1, waiting for transfers between devices, per_device(): lax.all_to_all(asked, ('rep', 'rows'), split_axis=0, concat_axis=0, tiled...  3.86 us
    pallas_call x1, Pallas kernels, per_device(): pl.pallas_call(normalize_kernel, out_shape=(jax.ShapeDtypeStruct((owners,...  3.64 us
    pallas_call x1, Pallas kernels, per_device(): pl.pallas_call(row_moments_kernel, out_shape=jax.ShapeDtypeStruct((2 * LA...  3.2 us
  transfers between devices with their start and end apart: 1, of which 1 were waited for; matrix products, arithmetic and copies ran while one was open for 0% of the time, Pallas kernels for 6%

profile of v1, /device:TPU:0, one launch (start us, length us, event | category | flops | bytes accessed | tf_op | source)
XLA Modules:
  0.0 57.0 jit_solution(2395999075880863732)
XLA Ops:
  0.6 0.8 %select_bitcast_fusion = s32[8,128]{1,0:T(8,128)S(1)} fusion(s32[1,8,128]{2,1,0:T(8,128)} %param.4, s32[8]{0:T(128)} %bitcast.14), kind=kLoop, calls=%fused_computation.1 | loop fusion | flops 2048 | bytes 8224 | tf_op jit(solution)/shard_map/broadcast_in_dim | solution.py:142
  1.4 0.6 %broadcast_in_dim.20 = s32[4,8,128]{2,1,0:T(8,128)} broadcast(s32[8,128]{1,0:T(8,128)S(1)} %select_bitcast_fusion), dimensions={1,2} | broadcast | bytes 20480 | tf_op jit(solution)/shard_map/broadcast_in_dim | solution.py:142
  2.0 7.3 %all-to-all-start = ((s32[32,1,128]{2,1,0:T(1,128)}), s32[32,1,128]{2,1,0:T(1,128)S(1)}, u32[]{:S(2)}, u32[]{:S(2)}) async-start(s32[32,1,128]{2,1,0:T(1,128)} %bitcast.2), calls=%async_computation | async-start | bytes 32768 | tf_op jit(solution)/shard_map/all_to_all | solution.py:143
  9.3 3.2 %row_moments.1.moments_ref = f32[32,128]{1,0:T(8,128)} custom-call(bf16[1024,512]{1,0:T(8,128)(2,1)} %table_ref.3), custom_call_target="tpu_custom_call" | custom-call | tf_op jit(solution)/shard_map/row_moments/pallas_call | solution.py:148
  12.5 3.9 %all-to-all-done = s32[32,1,128]{2,1,0:T(1,128)S(1)} async-done(((s32[32,1,128]{2,1,0:T(1,128)}), s32[32,1,128]{2,1,0:T(1,128)S(1)}, u32[]{:S(2)}, u32[]{:S(2)}) %all-to-all-start) | async-done | bytes 16416 | tf_op jit(solution)/shard_map/all_to_all | solution.py:143
  16.4 0.0 copy-start
  16.4 0.6 %dynamic-slice_bitcast_fusion.mine_ref = s32[8,128]{1,0:T(8,128)} fusion(s32[4,8,128]{2,1,0:T(8,128)S(1)} %bitcast.11, s32[]{:T(128)S(6)} %select_n.10), kind=kLoop, calls=%fused_computation | loop fusion | bytes 8196 | tf_op jit(solution)/shard_map/jit(dynamic_index_in_dim)/squeeze | solution.py:145
  17.0 0.0 copy-done
  17.0 4.9 %serve.1 = (bf16[8,520,128]{2,1,0:T(8,128)(2,1)}, s32[8,128]{1,0:T(8,128)}) custom-call(s32[8,128]{1,0:T(8,128)} %dynamic-slice_bitcast_fusion.mine_ref, s32[32,128]{1,0:T(8,128)} %bitcast.12, f32[32,128]{1,0:T(8,128)} %row_moments.1.moments_ref, bf16[1024,512]{1,0:T(8,128)(2,1)} %table_ref.3), custom_call_target="tpu_custom_call" | custom-call | tf_op jit(solution)/shard_map/serve/pallas_call | solution.py:155
  21.9 31.4 %all_to_all.16.received_ref = bf16[8,520,128]{2,1,0:T(8,128)(2,1)} all-to-all(bf16[8,520,128]{2,1,0:T(8,128)(2,1)} %get-tuple-element.7), channel_id=1, replica_groups=mesh['rows'=8,'rep'=4] {'rows'}, dimensions={0} | all-to-all | bytes 2129920 | tf_op jit(solution)/shard_map/all_to_all | solution.py:169
  53.3 3.6 %normalize.1 = (bf16[8,128,512]{2,1,0:T(8,128)(2,1)}, f32[2,2]{1,0:T(2,128)}) custom-call(s32[1,8]{1,0:T(1,128)} %used_ref.1, bf16[8,520,128]{2,1,0:T(8,128)(2,1)} %all_to_all.16.received_ref, f32[1,512]{1,0:T(1,128)} %bitcast.13), custom_call_target="tpu_custom_call" | custom-call | tf_op jit(solution)/shard_map/normalize/pallas_call | solution.py:170
Async XLA Ops:
  2.0 14.4 %all-to-all-start = ((s32[32,1,128]{2,1,0:T(1,128)}), s32[32,1,128]{2,1,0:T(1,128)S(1)}, u32[]{:S(2)}, u32[]{:S(2)}) async-start(s32[32,1,128]{2,1,0:T(1,128)} %bitcast.2), calls=%async_computation | async-start | bytes 32768 | tf_op jit(solution)/shard_map/all_to_all | solution.py:143
  16.4 0.6 %copy-start = (s32[32,1,128]{2,1,0:T(1,128)}, s32[32,1,128]{2,1,0:T(1,128)S(1)}, u32[]{:S(2)}) copy-start(s32[32,1,128]{2,1,0:T(1,128)S(1)} %all-to-all-done) | copy-start | bytes 49156
